TPU v7x, 32 devices: a whole 2x2x4 slice. The times are simulated.
32 devices in a mesh: dp: 8 (over z, x), tensor: 4 (over y, core).
Axes of the slice: x: 2, y: 2, z: 4, core: 2. Of those that a mesh axis runs over, the one named last changes fastest.
Arguments:
- latents: bfloat16 [32, 512, 1024], P(('dp', 'tensor')), may hold values from -6 to 6
- cotangent: bfloat16 [32, 512, 1024], P(('dp', 'tensor')), may hold values from -6 to 6
- counts: int32 [16], replicated, may hold values from 1 to 3, as said below
- assign: int32 [16], replicated, may hold values from 0 to 7, as said below
- pre_gain: float32 [1024], replicated, may hold values from 0.1 to 1.9
- pre_shift: float32 [1024], replicated, may hold values from -1.75 to 1.75
- w_query: bfloat16 [1024, 1024], P(None, 'tensor'), may hold values from -0.375 to 0.375
- b_query: float32 [1024], P('tensor'), may hold values from -3 to 3
- w_key: bfloat16 [1024, 1024], P(None, 'tensor'), may hold values from -0.1875 to 0.1875
- w_value: bfloat16 [1024, 1024], P(None, 'tensor'), may hold values from -0.1875 to 0.1875
- b_value: float32 [1024], P('tensor'), may hold values from -1.75 to 1.75
- w_out: bfloat16 [1024, 1024], P('tensor'), may hold values from -0.75 to 0.75
- b_out: float32 [1024], replicated, may hold values from -1.75 to 1.75
- mid_gain: float32 [1024], replicated, may hold values from 0.1 to 1.9
- mid_shift: float32 [1024], replicated, may hold values from -1.75 to 1.75
- w_up: bfloat16 [1024, 1024], P(None, 'tensor'), may hold values from -0.1875 to 0.1875
- b_up: float32 [1024], P('tensor'), may hold values from -1.75 to 1.75
- w_down: bfloat16 [1024, 1024], P('tensor'), may hold values from -0.25 to 0.25
- b_down: float32 [1024], replicated, may hold values from -1.75 to 1.75
Outputs:
- latents_out: bfloat16 [32, 512, 1024], P(('dp', 'tensor'))
- latents_grad: float32 [32, 512, 1024], P(('dp', 'tensor'))
- pregain_grad: float32 [1024], replicated
- preshift_grad: float32 [1024], replicated
- wquery_grad: float32 [1024, 1024], P(None, 'tensor')
- bquery_grad: float32 [1024], P('tensor')
- wkey_grad: float32 [1024, 1024], P(None, 'tensor')
- wvalue_grad: float32 [1024, 1024], P(None, 'tensor')
- bvalue_grad: float32 [1024], P('tensor')
- wout_grad: float32 [1024, 1024], P('tensor')
- bout_grad: float32 [1024], replicated
- midgain_grad: float32 [1024], replicated
- midshift_grad: float32 [1024], replicated
- wup_grad: float32 [1024, 1024], P(None, 'tensor')
- bup_grad: float32 [1024], P('tensor')
- wdown_grad: float32 [1024, 1024], P('tensor')
- bdown_grad: float32 [1024], replicated
Inputs may be any that keep to these rules, and one draw needn't show every extreme that they name: The counts of the 2 images of one data index add up to at most 4, and to exactly 4 on at least one data index. `assign`: each data index holds exactly 2 images.
All inputs are finite; a program needn't handle non-finite values.
Results may differ from a plain program's by a relative error of at most 0.017.
Values may be sent and summed in bfloat16 or wider, within the bound.
A program may use at most 128 MiB of HBM per device.

v0:
```python
from functools import partial
import math
import jax
import jax.numpy as jnp
from jax import lax
from jax.sharding import PartitionSpec as P

HEAD = 128
epsilon = 1e-05


def normalize(inputs, norm_gain, norm_shift):
    center = jnp.mean(inputs, axis=-1, keepdims=True)
    centered = inputs - center
    inverse = lax.rsqrt(jnp.mean(centered * centered, axis=-1, keepdims=True) + epsilon)
    scaled = centered * inverse
    return (scaled * norm_gain + norm_shift, scaled, inverse)


def norm_backward(upstream, scaled, inverse, norm_gain):
    weighted = upstream * norm_gain
    first_mean = jnp.mean(weighted, axis=-1, keepdims=True)
    second_mean = jnp.mean(weighted * scaled, axis=-1, keepdims=True)
    return inverse * (weighted - first_mean - scaled * second_mean)


def shards(
    latents,
    cotangent,
    counts,
    assign,
    pre_gain,
    pre_shift,
    w_query,
    b_query,
    w_key,
    w_value,
    b_value,
    w_out,
    b_out,
    mid_gain,
    mid_shift,
    w_up,
    b_up,
    w_down,
    b_down,
):
    f32, bf16 = (jnp.float32, jnp.bfloat16)
    crops, length, width = latents.shape
    tensor = lax.axis_size("tensor")
    heads = width // HEAD
    group_total = jnp.sum(jnp.where(assign == lax.axis_index("dp"), counts, 0))
    slot_ids = lax.axis_index("tensor") * crops + jnp.arange(crops, dtype=jnp.int32)
    live = jnp.repeat((slot_ids < group_total).astype(f32), length)[:, None]
    scaling = 1.0 / math.sqrt(HEAD)

    def dot(left, right, dims):
        return lax.dot_general(left, right, (dims, ((), ())), preferred_element_type=f32)

    columns = jnp.concatenate([w_query.T, w_key.T, w_value.T, w_out, w_up.T, w_down], axis=0)
    per = w_query.shape[1]
    gathered = lax.all_gather(columns, "tensor", axis=0, tiled=False).reshape(tensor, 6, per, width)
    wq, wk, wv, wo, wu, wd = [gathered[:, i].reshape(tensor * per, width) for i in range(6)]
    bias = lax.all_gather(jnp.stack([b_query, b_value, b_up]), "tensor", axis=1, tiled=True)
    rows = latents.astype(f32).reshape(crops * length, width)
    normed, scaled, inverse = normalize(rows, pre_gain, pre_shift)
    normed = normed.astype(bf16)
    q = (dot(normed, wq, ((1,), (1,))) + bias[0]).astype(bf16)
    k = dot(normed, wk, ((1,), (1,))).astype(bf16)
    v = (dot(normed, wv, ((1,), (1,))) + bias[1]).astype(bf16)
    split = lambda a: a.reshape(crops, length, heads, HEAD)
    q4, k4, v4 = (split(q), split(k), split(v))
    ein = partial(jnp.einsum, preferred_element_type=f32)
    probs = jax.nn.softmax(ein("cqhd,ckhd->chqk", q4, k4) * scaling, axis=-1)
    low = probs.astype(bf16)
    mixed = ein("chqk,ckhd->cqhd", low, v4).astype(bf16).reshape(crops * length, width)
    hidden = rows + (dot(mixed, wo, ((1,), (0,))) + b_out)
    normed2, scaled2, inverse2 = normalize(hidden, mid_gain, mid_shift)
    normed2 = normed2.astype(bf16)
    upward = dot(normed2, wu, ((1,), (1,))) + bias[2]
    act32, gelu_pull = jax.vjp(partial(jax.nn.gelu, approximate=True), upward)
    act = act32.astype(bf16)
    result = hidden + (dot(act, wd, ((1,), (0,))) + b_down)
    latents_out = (result * live).astype(bf16).reshape(latents.shape)
    gy = cotangent.reshape(crops * length, width) * live.astype(bf16)
    g_wd = dot(act, gy, ((0,), (0,)))
    gu = gelu_pull(dot(gy, wd, ((1,), (1,))))[0].astype(bf16)
    g_wu = dot(gu, normed2, ((0,), (0,)))
    gn2 = dot(gu, wu, ((1,), (0,)))
    gh = gy.astype(f32) + norm_backward(gn2, scaled2, inverse2, mid_gain)
    ga = gh.astype(bf16)
    g_wo = dot(mixed, ga, ((0,), (0,)))
    go = split(dot(ga, wo, ((1,), (1,))).astype(bf16))
    gp = ein("cqhd,ckhd->chqk", go, v4)
    gs = (probs * (gp - jnp.sum(probs * gp, axis=-1, keepdims=True))).astype(bf16)
    flat = lambda a: a.astype(bf16).reshape(crops * length, width)
    gq = flat(ein("chqk,ckhd->cqhd", gs, k4) * scaling)
    gk = flat(ein("chqk,cqhd->ckhd", gs, q4) * scaling)
    gv = flat(ein("chqk,cqhd->ckhd", low, go))
    g_wq, g_wk, g_wv = [dot(a, normed, ((0,), (0,))) for a in (gq, gk, gv)]
    gn1 = dot(gq, wq, ((1,), (0,))) + dot(gk, wk, ((1,), (0,))) + dot(gv, wv, ((1,), (0,)))
    latents_grad = (gh + norm_backward(gn1, scaled, inverse, pre_gain)).reshape(latents.shape)

    def total(parts):
        stacked = jnp.stack([p.astype(bf16).reshape(tensor, per, width) for p in parts], axis=1)
        part = lax.psum_scatter(stacked, "tensor", scatter_dimension=0, tiled=True)
        return lax.psum(part, "dp")[0].astype(f32)

    s_wd, s_wu, s_wo = total((g_wd, g_wu, g_wo))
    s_wq, s_wk, s_wv = total((g_wq, g_wk, g_wv))
    col = lambda a: jnp.sum(a, axis=0, dtype=f32)
    sums = lax.psum(
        jnp.stack(
            [
                col(gn1 * scaled),
                col(gn1),
                col(ga),
                col(gn2 * scaled2),
                col(gn2),
                col(gy),
                col(gq),
                col(gv),
                col(gu),
            ]
        ),
        ("dp", "tensor"),
    )
    mine = lax.dynamic_slice_in_dim(sums[6:], lax.axis_index("tensor") * per, per, axis=1)
    return (
        latents_out,
        latents_grad,
        sums[0],
        sums[1],
        s_wq.T,
        mine[0],
        s_wk.T,
        s_wv.T,
        mine[1],
        s_wo,
        sums[2],
        sums[3],
        sums[4],
        s_wu.T,
        mine[2],
        s_wd,
        sums[5],
    )


def solution(mesh):
    return jax.shard_map(
        shards,
        mesh=mesh,
        in_specs=(
            P(("dp", "tensor"), None, None),
            P(("dp", "tensor"), None, None),
            P(),
            P(),
            P(),
            P(),
            P(None, "tensor"),
            P("tensor"),
            P(None, "tensor"),
            P(None, "tensor"),
            P("tensor"),
            P("tensor", None),
            P(),
            P(),
            P(),
            P(None, "tensor"),
            P("tensor"),
            P("tensor", None),
            P(),
        ),
        out_specs=(
            P(("dp", "tensor"), None, None),
            P(("dp", "tensor"), None, None),
            P(),
            P(),
            P(None, "tensor"),
            P("tensor"),
            P(None, "tensor"),
            P(None, "tensor"),
            P("tensor"),
            P("tensor", None),
            P(),
            P(),
            P(),
            P(None, "tensor"),
            P("tensor"),
            P("tensor", None),
            P(),
        ),
        check_vma=False,
    )
```

profile of v0, /device:TPU:0, one launch (start us, length us, event | category | flops | bytes accessed | tf_op | source)
XLA Modules:
  0.0 419.4 jit_solution(4079117353360037108)
XLA Ops:
  7.3 1.3 copy.36
  8.6 1.2 copy.37
  16.9 6.3 %all_gather.11 = f32[3,1024]{1,0:T(4,128)S(1)} all-gather(f32[3,256]{1,0:T(4,128)S(1)} %pad_maximum_fusion.2), channel_id=1, replica_groups=mesh['dp'=8,'tensor'=4] {'tensor'}, dimensions={1}, use_global_device_ids=true | all-gather | bytes 15360 | tf_op jit(solution)/shard_map/all_gather | solution.py:64
  23.8 76.6 %all-gather.3.cloned.1.call-done = bf16[6144,1024]{1,0:T(8,128)(2,1)} async-done(((bf16[1536,1024]{1,0:T(8,128)(2,1)}), bf16[6144,1024]{1,0:T(8,128)(2,1)}) %all-gather.3.cloned.1.call-update) | async-done | bytes 12582928 | tf_op jit(solution)/shard_map/all_gather | solution.py:62
  100.4 9.0 %fusion.70 = (bf16[4,1,256,1024]{3,2,1,0:T(8,128)(2,1)}, bf16[4,1,256,1024]{3,2,1,0:T(8,128)(2,1)}, bf16[4,1,256,1024]{3,2,1,0:T(8,128)(2,1)}, bf16[4,1,256,1024...) fusion(bf16[4,6,256,1024]{3,2,1,0:T(8,128)(2,1)} %bitcast.191), kind=kLoop, calls=%fused_computation.118 | loop fusion | bytes 25165824 | tf_op jit(solution)/shard_map/slice | solution.py:63
  109.4 2.3 add_convert_fusion.1
  111.7 2.3 copy.63
  114.0 2.9 convolution_convert_fusion.7
  117.5 4.3 %fusion.40 = bf16[64,8,8,128]{3,2,1,0:T(8,128)(2,1)} fusion(bf16[1024,1024]{1,0:T(8,128)(2,1)} %bitcast.208, f32[1024]{0:T(1024)S(1)} %bitcast.240, bf16[1,512,1024]{2,1,0:T(8,128)(2,1)S(1)} %copy-done.1, f32[1024]{0:T(1024)S(1)} %copy-done.31, f32[1024]{0:T(1024)S(1)} %copy-done.24, f32[512]{0:T(512)S(1)} %add_rsqrt_fusion.1, ...), kind=kOutput, calls=%fused_computation.74 | convolution fusion | flops 1077936128 | bytes 4210688 | tf_op jit(solution)/shard_map/dot_general | solution.py:58
  121.8 5.5 %fusion.74 = (f32[8,512]{1,0:T(8,128)S(1)}, f32[8,512,512]{1,2,0:T(8,128)}) fusion(bf16[512,8,128]{0,2,1:T(8,128)(2,1)S(1)} %bitcast.203, bf16[512,8,128]{0,2,1:T(8,128)(2,1)S(1)} %bitcast.204), kind=kOutput, calls=%fused_computation.122 | convolution fusion | flops 543162880 | bytes 10502144 | tf_op jit(solution)/shard_map/sub | solution.py:74
  127.3 4.7 %fusion.34 = bf16[8,128,512]{2,1,0:T(8,128)(2,1)S(1)} fusion(bf16[64,8,8,128]{3,2,1,0:T(8,128)(2,1)} %fusion.40, f32[8,512,512]{1,2,0:T(8,128)} %get-tuple-element.72, f32[8,512]{1,0:T(8,128)S(1)} %get-tuple-element.71), kind=kOutput, calls=%fused_computation.70 | convolution fusion | flops 541589504 | bytes 10502144 | tf_op jit(solution)/shard_map/chqk,ckhd->cqhd/dot_general | solution.py:76
  132.0 1.4 fusion.75
  133.8 1.2 copy-done.15
  135.0 1.3 fusion.63
  136.4 1.7 convolution_convert_fusion.2
  138.7 2.5 convert_reduce_fusion.2
  141.2 1.8 multiply_reduce_fusion.2
  143.0 1.5 convolution_convert_fusion.1
  144.5 0.9 convert_reduce_fusion.5
  145.5 1.3 convolution_convert_fusion
  146.8 3.4 pad_maximum_fusion.1
  150.2 4.5 %convolution_convert_fusion.6 = bf16[512,1024]{1,0:T(8,128)(2,1)} fusion(bf16[1024,1024]{1,0:T(8,128)(2,1)} %bitcast.196, f32[512,1024]{1,0:T(8,128)} %copy-done.5), kind=kOutput, calls=%fused_computation.72 | convolution fusion | flops 1074790400 | bytes 5242880 | tf_op jit(solution)/shard_map/dot_general | solution.py:58
  154.7 2.5 copy.65
  157.2 7.1 %convert_reduce_fusion.3 = (f32[8,128]{1,0:T(8,128)S(1)}, bf16[8,128,512]{2,1,0:T(8,128)(2,1)S(1)}) fusion(bf16[512,8,128]{0,2,1:T(8,128)(2,1)} %bitcast.218, f32[8,512,512]{1,2,0:T(8,128)} %get-tuple-element.72, f32[8,512]{1,0:T(8,128)S(1)} %get-tuple-element.71), kind=kOutput, calls=%fused_computation.43 | convolution fusion | flops 542637056 | bytes 10506240 | tf_op jit(solution)/shard_map/chqk,cqhd->ckhd/dot_general | solution.py:99
  164.3 2.7 convolution_convert_fusion.3
  167.0 3.9 copy.54
  170.9 6.2 %multiply_reduce_fusion = (f32[8,512]{1,0:T(8,128)S(1)}, f32[8,512,512]{1,2,0:T(8,128)S(1)}) fusion(f32[8,512,512]{1,2,0:T(8,128)} %get-tuple-element.72, f32[8,512]{1,0:T(8,128)S(1)} %get-tuple-element.71, bf16[512,8,128]{0,2,1:T(8,128)(2,1)} %bitcast.219, bf16[64,8,8,128]{3,2,1,0:T(8,128)(2,1)} %fusion.40), kind=kOutput, calls=%fused_computation.2 | convolution fusion | flops 543158272 | bytes 18907136 | tf_op jit(solution)/shard_map/cqhd,ckhd->chqk/dot_general | solution.py:94
  177.1 4.5 %multiply_convert_fusion = bf16[8,512,512]{1,2,0:T(8,128)(2,1)S(1)} fusion(f32[8,512,512]{1,2,0:T(8,128)S(1)} %get-tuple-element.77, f32[8,512]{1,0:T(8,128)S(1)} %get-tuple-element.76, f32[8,512,512]{1,2,0:T(8,128)} %get-tuple-element.72, f32[8,512]{1,0:T(8,128)S(1)} %get-tuple-element.71), kind=kLoop, calls=%fused_computation.1 | loop fusion | flops 8388608 | bytes 21004288 | tf_op jit(solution)/shard_map/convert_element_type | solution.py:95
  182.5 1.1 copy-done
  183.6 2.7 convolution_convert_fusion.5
  186.3 4.0 copy.52
  190.3 4.0 multiply_convert_fusion.1
  194.3 2.8 convolution_convert_fusion.4
  197.1 4.0 copy.53
  201.0 6.5 %pad_maximum_fusion = bf16[4,3,256,1024]{2,3,1,0:T(8,128)(2,1)} fusion(bf16[4,1,256,1024]{2,3,1,0:T(8,128)(2,1)} %copy.54, bf16[4,1,256,1024]{2,3,1,0:T(8,128)(2,1)} %copy.53, bf16[4,1,256,1024]{2,3,1,0:T(8,128)(2,1)} %copy.52), kind=kLoop, calls=%fused_computation.6 | loop fusion | flops 6291456 | bytes 12582912 | tf_op jit(solution)/shard_map/stack | solution.py:105
  207.8 1.4 reduce-scatter.5.cloned.1.call-done
  209.2 61.4 %reduce-scatter.3.cloned.1.call-done = bf16[1,3,256,1024]{2,3,1,0:T(8,128)(2,1)} async-done(((bf16[4,3,256,1024]{2,3,1,0:T(8,128)(2,1)}), bf16[1,3,256,1024]{2,3,1,0:T(8,128)(2,1)}) %reduce-scatter.3.cloned.1.call-update) | async-done | bytes 1572880 | tf_op jit(solution)/shard_map/reduce_scatter | solution.py:106
  270.6 3.3 fusion.77
  274.0 1.3 fusion.76
  275.8 3.3 fusion.17
  279.2 42.9 %psum.21 = f32[9,1024]{1,0:T(8,128)S(1)} all-reduce(f32[9,1024]{1,0:T(8,128)S(1)} %stack.61), channel_id=1, replica_groups=mesh['dp'=8,'tensor'=4] {'dp','tensor'}, use_global_device_ids=true, to_apply=%region_21.22 | all-reduce | flops 9216 | bytes 73728 | tf_op jit(solution)/shard_map/psum | solution.py:112
  323.5 4.4 %fusion.16 = f32[1,512,1024]{2,1,0:T(8,128)} fusion(f32[512,1024]{1,0:T(8,128)} %copy-done.5, bf16[1,512,1024]{2,1,0:T(8,128)(2,1)S(1)} %copy-done.1, f32[512,1024]{1,0:T(8,128)} %get-tuple-element.78, f32[512]{0:T(512)S(1)} %broadcast_multiply_fusion, f32[512]{0:T(512)S(1)} %broadcast_multiply_fusion.1, f32[1024]{0:T(1024)S(1)} %copy-done.24, ...), kind=kLoop, calls=%fused_computation.28 | loop fusion | flops 4718592 | bytes 7352320 | tf_op jit(solution)/shard_map/reshape | solution.py:102
  327.9 2.6 fusion.41
  330.5 73.5 %all-reduce.3.cloned.1.call-done = (bf16[1,3,256,1024]{2,3,1,0:T(8,128)(2,1)}, bf16[1,3,256,1024]{3,2,1,0:T(8,128)(2,1)}) async-done(((bf16[1,3,256,1024]{2,3,1,0:T(8,128)(2,1)}, bf16[1,3,256,1024]{3,2,1,0:T(8,128)(2,1)}), (bf16[1,3,256,1024]{2,3,1,0:T(8,128)(2,1)}, bf16[1,3,256,1024]{3,2,1,0:T(8,128)(2,1)})) %all-reduce.3.cloned.1.call-update) | async-done | bytes 3145744 | tf_op jit(solution)/shard_map/psum | solution.py:107
  403.9 1.7 convert_element_type.173
  405.6 1.7 slice_bitcast_fusion.3
  408.4 1.8 slice_bitcast_fusion
  410.2 2.5 copy.58
  (108 shorter events, 12.7 us)
Async XLA Ops:
  7.2 2.7 copy-start.18
  7.2 2.9 copy-start.19
  7.2 93.2 %all-gather.3.cloned.1.call-start = ((), (), s32[]{:S(2)}) async-start(), calls=%async_computation.4 | async-start | bytes 15728640 | tf_op jit(solution)/shard_map/all_gather | solution.py:62
  10.1 2.8 copy-start.20
  11.2 3.4 copy-start.21
  14.5 1.0 copy-start.28
  14.5 1.0 copy-start.29
  14.5 2.3 copy-start.25
  14.5 2.3 copy-start.26
  14.6 2.3 copy-start.27
  14.6 8.6 %copy-start.1 = (bf16[1,512,1024]{2,1,0:T(8,128)(2,1)S(1)}, bf16[1,512,1024]{2,1,0:T(8,128)(2,1)}, u32[]{:S(2)}) copy-start(bf16[1,512,1024]{2,1,0:T(8,128)(2,1)} %param.19) | copy-start | bytes 3145732
  15.5 193.7 %reduce-scatter.5.cloned.1.call-start = ((), (), s32[]{:S(2)}) async-start(), calls=%async_computation.3 | async-start | bytes 7864320 | tf_op jit(solution)/shard_map/reduce_scatter | solution.py:106
  100.4 9.0 %copy-start.24 = (f32[1024]{0:T(1024)S(1)}, f32[1024]{0:T(1024)}, u32[]{:S(2)}) copy-start(f32[1024]{0:T(1024)} %param.23) | copy-start | bytes 12292
  100.4 9.0 %copy-start.31 = (f32[1024]{0:T(1024)S(1)}, f32[1024]{0:T(1024)}, u32[]{:S(2)}) copy-start(f32[1024]{0:T(1024)} %param.24) | copy-start | bytes 12292
  109.4 2.3 copy-start.2
  117.5 4.3 %copy-start.10 = (bf16[512,1024]{0,1:T(8,128)(2,1)}, bf16[512,1024]{0,1:T(8,128)(2,1)S(1)}, u32[]{:S(2)}) copy-start(bf16[512,1024]{0,1:T(8,128)(2,1)S(1)} %copy.64) | copy-start | bytes 3145732
  117.5 4.3 %copy-start.9 = (bf16[512,1024]{0,1:T(8,128)(2,1)S(1)}, bf16[512,1024]{0,1:T(8,128)(2,1)}, u32[]{:S(2)}) copy-start(bf16[512,1024]{0,1:T(8,128)(2,1)} %copy.63) | copy-start | bytes 3145732
  127.3 4.8 %copy-start.4 = (bf16[4,1,256,1024]{3,2,1,0:T(8,128)(2,1)S(1)}, bf16[4,1,256,1024]{3,2,1,0:T(8,128)(2,1)}, u32[]{:S(2)}) copy-start(bf16[4,1,256,1024]{3,2,1,0:T(8,128)(2,1)} %get-tuple-element.48) | copy-start | bytes 6291460
  127.3 4.8 %copy-start.22 = (f32[1024]{0:T(1024)S(1)}, f32[1024]{0:T(1024)}, u32[]{:S(2)}) copy-start(f32[1024]{0:T(1024)} %param.31) | copy-start | bytes 12292
  133.4 1.6 copy-start.15
  133.4 1.6 copy-start.23
  133.4 1.6 copy-start.30
  135.0 1.4 copy-start.17
  136.4 1.7 copy-start.35
  136.4 2.3 copy-start.12
  145.5 1.3 copy-start.5
  150.2 120.4 %reduce-scatter.3.cloned.1.call-start = ((), (), s32[]{:S(2)}) async-start(), calls=%async_computation.2 | async-start | bytes 7864320 | tf_op jit(solution)/shard_map/reduce_scatter | solution.py:106
  164.3 2.7 copy-start.33
  177.1 4.5 %copy-start.11 = (bf16[512,1024]{0,1:T(8,128)(2,1)S(1)}, bf16[512,1024]{0,1:T(8,128)(2,1)}, u32[]{:S(2)}) copy-start(bf16[512,1024]{0,1:T(8,128)(2,1)} %copy-done.10) | copy-start | bytes 3145732
  181.6 1.9 copy-start
  183.6 2.7 copy-start.6
  194.3 2.8 copy-start.8
  207.5 196.4 %all-reduce.3.cloned.1.call-start = ((), (), s32[]{:S(2)}) async-start(), calls=%async_computation.5 | async-start | bytes 6291456 | tf_op jit(solution)/shard_map/psum | solution.py:107
  270.6 3.4 copy-start.3
  270.6 3.4 copy-start.7
  274.0 1.6 copy-start.14
  274.0 1.8 copy-start.34
  323.5 4.4 %copy-start.13 = (bf16[4,1,256,1024]{3,2,1,0:T(8,128)(2,1)S(1)}, bf16[4,1,256,1024]{3,2,1,0:T(8,128)(2,1)}, u32[]{:S(2)}) copy-start(bf16[4,1,256,1024]{3,2,1,0:T(8,128)(2,1)} %get-tuple-element.47) | copy-start | bytes 6291460
  323.5 4.4 %copy-start.32 = (f32[1024]{0:T(1024)S(1)}, f32[1024]{0:T(1024)}, u32[]{:S(2)}) copy-start(f32[1024]{0:T(1024)} %param.37) | copy-start | bytes 12292
  323.5 4.4 %copy-start.36 = (f32[512,1024]{1,0:T(8,128)S(1)}, f32[512,1024]{1,0:T(8,128)}, u32[]{:S(2)}) copy-start(f32[512,1024]{1,0:T(8,128)} %copy-done.35) | copy-start | bytes 6291460
  405.6 2.4 copy-start.16
Sparse Core Ops, SparseCore 0:
  15.6 84.7 all-gather.2
  150.3 58.8 reduce-scatter.4
  211.7 58.8 reduce-scatter.2
  274.1 129.8 all-reduce.2
where the time goes:
time: 426 us; the launch traced here: 419 us
  waiting for transfers between devices  213 us (50%)
  matrix products  72.4 us (17%)
  blocking collectives  49.2 us (12%)
  local copies, waits for them, and re-layouts  45.9 us (11%)
  other arithmetic  23.3 us (5%)
  between operations  15.2 us (4%)
    all_gather x1, waiting for transfers between devices, shards(): lax.all_gather(columns, 'tensor', axis=0, tiled=False)  76.6 us
    psum x1, waiting for transfers between devices, total(): return lax.psum(part, 'dp')[0].astype(f32)  73.5 us
    reduce_scatter x2, waiting for transfers between devices, total(): part = lax.psum_scatter(stacked, 'tensor', scatter_dimension=0, tiled=True)  62.8 us
    dot_general x18, matrix products, dot(): lax.dot_general(left, right, (dims, ((), ())), preferred_element_type=f32)  44 us
    psum x1, blocking collectives, shards(): lax.psum(jnp.stack([col(gn1 * scaled), col(gn1), col(ga), col(gn2 * scale...  42.9 us
    unnamed x84, local copies, waits for them, and re-layouts  14.1 us
    another operation x3, local copies, waits for them, and re-layouts, total(): jnp.stack([p.astype(bf16).reshape(tensor, per, width) for p in parts], ax...  11.8 us
    another operation x2, other arithmetic, total(): jnp.stack([p.astype(bf16).reshape(tensor, per, width) for p in parts], ax...  9.82 us
  transfers between devices with their start and end apart: 4, of which 4 were waited for; matrix products, arithmetic and copies ran while one was open for 18% of the time, Pallas kernels for 0%

commit v1 on v0

--- a/solution.py
+++ b/solution.py
@@ -109,22 +109,20 @@
     s_wd, s_wu, s_wo = total((g_wd, g_wu, g_wo))
     s_wq, s_wk, s_wv = total((g_wq, g_wk, g_wv))
     col = lambda a: jnp.sum(a, axis=0, dtype=f32)
-    sums = lax.psum(
-        jnp.stack(
-            [
-                col(gn1 * scaled),
-                col(gn1),
-                col(ga),
-                col(gn2 * scaled2),
-                col(gn2),
-                col(gy),
-                col(gq),
-                col(gv),
-                col(gu),
-            ]
-        ),
-        ("dp", "tensor"),
+    xx = jnp.stack(
+        [
+            col(gn1 * scaled),
+            col(gn1),
+            col(ga),
+            col(gn2 * scaled2),
+            col(gn2),
+            col(gy),
+            col(gq),
+            col(gv),
+            col(gu),
+        ]
     )
+    sums = lax.all_gather(xx, ("dp", "tensor")).sum(axis=0)
     mine = lax.dynamic_slice_in_dim(sums[6:], lax.axis_index("tensor") * per, per, axis=1)
     return (
         latents_out,

time: 426 us -> 484 us (1.14)
  waiting for transfers between devices: 213 us -> 310 us
  blocking collectives: 49.2 us -> 6.27 us
    psum x1, waiting for transfers between devices: 73.5 us -> 128 us  [total(): return lax.psum(part, 'dp')[0].astype(f32)]
    all_gather x0 -> x1, waiting for transfers between devices: none -> 52.5 us  [shards(): sums = lax.all_gather(xx, ('dp', 'tensor')).sum(axis=0)]
    psum x1 -> x0, blocking collectives: 42.9 us -> none  [shards(): lax.psum(jnp.stack([col(gn1 * scaled), col(gn1), col(ga), col(gn2 * scale...]
    reduce_scatter x2, waiting for transfers between devices: 62.8 us -> 52.9 us  [total(): part = lax.psum_scatter(stacked, 'tensor', scatter_dimension=0, tiled=True)]
  transfers between devices with their start and end apart: 4 -> 5, of which waited for: 4 -> 4; matrix products, arithmetic and copies ran while one was open for 18% -> 16% of each run, Pallas kernels for 0% -> 0%
where the time goes in v1:
time: 484 us; the launch traced here: 477 us
  waiting for transfers between devices  310 us (64%)
  matrix products  72.4 us (15%)
  local copies, waits for them, and re-layouts  47.1 us (10%)
  other arithmetic  25.1 us (5%)
  between operations  15.3 us (3%)
  blocking collectives  6.27 us (1%)
    psum x1, waiting for transfers between devices, total(): return lax.psum(part, 'dp')[0].astype(f32)  128 us
    all_gather x1, waiting for transfers between devices, shards(): lax.all_gather(columns, 'tensor', axis=0, tiled=False)  76.6 us
    reduce_scatter x2, waiting for transfers between devices, total(): part = lax.psum_scatter(stacked, 'tensor', scatter_dimension=0, tiled=True)  52.9 us
    all_gather x1, waiting for transfers between devices, shards(): sums = lax.all_gather(xx, ('dp', 'tensor')).sum(axis=0)  52.5 us
    dot_general x18, matrix products, dot(): lax.dot_general(left, right, (dims, ((), ())), preferred_element_type=f32)  44.1 us
    unnamed x84, local copies, waits for them, and re-layouts  14.1 us
    another operation x3, local copies, waits for them, and re-layouts, total(): jnp.stack([p.astype(bf16).reshape(tensor, per, width) for p in parts], ax...  11.8 us
    another operation x2, other arithmetic, total(): jnp.stack([p.astype(bf16).reshape(tensor, per, width) for p in parts], ax...  9.82 us
  transfers between devices with their start and end apart: 5, of which 4 were waited for; matrix products, arithmetic and copies ran while one was open for 16% of the time, Pallas kernels for 0%

profile of v1, /device:TPU:0, one launch (start us, length us, event | category | flops | bytes accessed | tf_op | source)
XLA Modules:
  0.0 477.0 jit_solution(2687523989882324035)
XLA Ops:
  7.3 1.3 copy.59
  8.6 1.2 copy.60
  16.9 6.3 %all_gather.17 = f32[3,1024]{1,0:T(4,128)S(1)} all-gather(f32[3,256]{1,0:T(4,128)S(1)} %pad_maximum_fusion.2), channel_id=1, replica_groups=mesh['dp'=8,'tensor'=4] {'tensor'}, dimensions={1}, use_global_device_ids=true | all-gather | bytes 15360 | tf_op jit(solution)/shard_map/all_gather | solution.py:64
  23.8 76.6 %all-gather.6.cloned.1.call-done = bf16[6144,1024]{1,0:T(8,128)(2,1)} async-done(((bf16[1536,1024]{1,0:T(8,128)(2,1)}), bf16[6144,1024]{1,0:T(8,128)(2,1)}) %all-gather.6.cloned.1.call-update) | async-done | bytes 12582928 | tf_op jit(solution)/shard_map/all_gather | solution.py:62
  100.4 8.9 %fusion.70 = (bf16[4,1,256,1024]{3,2,1,0:T(8,128)(2,1)}, bf16[4,1,256,1024]{3,2,1,0:T(8,128)(2,1)}, bf16[4,1,256,1024]{3,2,1,0:T(8,128)(2,1)}, bf16[4,1,256,1024...) fusion(bf16[4,6,256,1024]{3,2,1,0:T(8,128)(2,1)} %bitcast.192), kind=kLoop, calls=%fused_computation.118 | loop fusion | bytes 25165824 | tf_op jit(solution)/shard_map/slice | solution.py:63
  109.4 2.3 add_convert_fusion.1
  111.7 2.3 copy.86
  113.9 2.9 convolution_convert_fusion.7
  117.4 4.3 fusion.40
  121.7 5.5 %fusion.74 = (f32[8,512]{1,0:T(8,128)S(1)}, f32[8,512,512]{1,2,0:T(8,128)}) fusion(bf16[512,8,128]{0,2,1:T(8,128)(2,1)S(1)} %bitcast.204, bf16[512,8,128]{0,2,1:T(8,128)(2,1)S(1)} %bitcast.205), kind=kOutput, calls=%fused_computation.122 | convolution fusion | flops 543162880 | bytes 10502144 | tf_op jit(solution)/shard_map/sub | solution.py:74
  127.2 4.7 fusion.34
  132.0 1.4 fusion.75
  133.8 1.2 copy-done.15
  135.0 1.3 fusion.63
  136.3 1.7 convolution_convert_fusion.2
  138.7 2.5 convert_reduce_fusion.2
  141.2 1.8 multiply_reduce_fusion.2
  143.0 1.5 convolution_convert_fusion.1
  145.4 1.3 convolution_convert_fusion
  146.7 3.4 pad_maximum_fusion.1
  150.2 4.5 convolution_convert_fusion.6
  154.7 2.5 copy.88
  157.1 7.1 %convert_reduce_fusion.3 = (f32[8,128]{1,0:T(8,128)S(1)}, bf16[8,128,512]{2,1,0:T(8,128)(2,1)S(1)}) fusion(bf16[512,8,128]{0,2,1:T(8,128)(2,1)} %bitcast.219, f32[8,512,512]{1,2,0:T(8,128)} %get-tuple-element.89, f32[8,512]{1,0:T(8,128)S(1)} %get-tuple-element.88), kind=kOutput, calls=%fused_computation.43 | convolution fusion | flops 542637056 | bytes 10506240 | tf_op jit(solution)/shard_map/chqk,cqhd->ckhd/dot_general | solution.py:99
  164.2 2.7 convolution_convert_fusion.3
  166.9 3.9 copy.77
  170.9 6.2 %multiply_reduce_fusion = (f32[8,512]{1,0:T(8,128)S(1)}, f32[8,512,512]{1,2,0:T(8,128)S(1)}) fusion(f32[8,512,512]{1,2,0:T(8,128)} %get-tuple-element.89, f32[8,512]{1,0:T(8,128)S(1)} %get-tuple-element.88, bf16[512,8,128]{0,2,1:T(8,128)(2,1)} %bitcast.220, bf16[64,8,8,128]{3,2,1,0:T(8,128)(2,1)} %fusion.40), kind=kOutput, calls=%fused_computation.2 | convolution fusion | flops 543158272 | bytes 18907136 | tf_op jit(solution)/shard_map/cqhd,ckhd->chqk/dot_general | solution.py:94
  177.1 4.5 multiply_convert_fusion
  182.4 1.1 copy-done
  183.5 2.7 convolution_convert_fusion.5
  186.3 4.0 copy.75
  190.2 4.0 multiply_convert_fusion.1
  194.3 2.8 convolution_convert_fusion.4
  197.0 4.0 copy.76
  201.0 6.5 %pad_maximum_fusion = bf16[4,3,256,1024]{2,3,1,0:T(8,128)(2,1)} fusion(bf16[4,1,256,1024]{2,3,1,0:T(8,128)(2,1)} %copy.77, bf16[4,1,256,1024]{2,3,1,0:T(8,128)(2,1)} %copy.76, bf16[4,1,256,1024]{2,3,1,0:T(8,128)(2,1)} %copy.75), kind=kLoop, calls=%fused_computation.6 | loop fusion | flops 6291456 | bytes 12582912 | tf_op jit(solution)/shard_map/stack | solution.py:105
  207.8 3.5 fusion.77
  211.3 1.3 fusion.76
  213.1 3.2 fusion.17
  216.4 1.3 stack.61
  217.7 52.8 %reduce-scatter.3.cloned.1.call-done = bf16[1,3,256,1024]{2,3,1,0:T(8,128)(2,1)} async-done(((bf16[4,3,256,1024]{2,3,1,0:T(8,128)(2,1)}), bf16[1,3,256,1024]{2,3,1,0:T(8,128)(2,1)}) %reduce-scatter.3.cloned.1.call-update) | async-done | bytes 1572880 | tf_op jit(solution)/shard_map/reduce_scatter | solution.py:106
  270.7 4.4 fusion.16
  275.1 2.6 fusion.41
  277.6 52.5 %all-gather.8.cloned.1.call-done = f32[32,9,1024]{2,1,0:T(8,128)} async-done(((f32[1,9,1024]{2,1,0:T(8,128)}), f32[32,9,1024]{2,1,0:T(8,128)}) %all-gather.8.cloned.1.call-update) | async-done | bytes 1179664 | tf_op jit(solution)/shard_map/all_gather | solution.py:125
  330.2 1.7 reduce_sum.209
  333.2 128.3 %all-reduce.3.cloned.1.call-done = (bf16[1,3,256,1024]{2,3,1,0:T(8,128)(2,1)}, bf16[1,3,256,1024]{3,2,1,0:T(8,128)(2,1)}) async-done(((bf16[1,3,256,1024]{2,3,1,0:T(8,128)(2,1)}, bf16[1,3,256,1024]{3,2,1,0:T(8,128)(2,1)}), (bf16[1,3,256,1024]{2,3,1,0:T(8,128)(2,1)}, bf16[1,3,256,1024]{3,2,1,0:T(8,128)(2,1)})) %all-reduce.3.cloned.1.call-update) | async-done | bytes 3145744 | tf_op jit(solution)/shard_map/psum | solution.py:107
  461.5 1.7 convert_element_type.173
  463.2 1.7 slice_bitcast_fusion.3
  465.9 1.8 slice_bitcast_fusion
  467.7 2.5 copy.81
  (111 shorter events, 13.7 us)
Async XLA Ops:
  7.2 2.7 copy-start.18
  7.2 2.9 copy-start.19
  7.2 93.2 %all-gather.6.cloned.1.call-start = ((), (), s32[]{:S(2)}) async-start(), calls=%async_computation.4 | async-start | bytes 15728640 | tf_op jit(solution)/shard_map/all_gather | solution.py:62
  10.1 2.8 copy-start.20
  11.2 3.4 copy-start.21
  14.5 1.0 copy-start.28
  14.5 1.0 copy-start.29
  14.5 2.3 copy-start.25
  14.5 2.3 copy-start.26
  14.6 2.3 copy-start.27
  14.6 8.6 %copy-start.1 = (bf16[1,512,1024]{2,1,0:T(8,128)(2,1)S(1)}, bf16[1,512,1024]{2,1,0:T(8,128)(2,1)}, u32[]{:S(2)}) copy-start(bf16[1,512,1024]{2,1,0:T(8,128)(2,1)} %param.19) | copy-start | bytes 3145732
  15.5 202.3 %reduce-scatter.5.cloned.1.call-start = ((), (), s32[]{:S(2)}) async-start(), calls=%async_computation.3 | async-start | bytes 7864320 | tf_op jit(solution)/shard_map/reduce_scatter | solution.py:106
  100.4 8.9 %copy-start.24 = (f32[1024]{0:T(1024)S(1)}, f32[1024]{0:T(1024)}, u32[]{:S(2)}) copy-start(f32[1024]{0:T(1024)} %param.23) | copy-start | bytes 12292
  100.4 9.0 %copy-start.31 = (f32[1024]{0:T(1024)S(1)}, f32[1024]{0:T(1024)}, u32[]{:S(2)}) copy-start(f32[1024]{0:T(1024)} %param.24) | copy-start | bytes 12292
  109.4 2.3 copy-start.2
  117.4 4.3 copy-start.10
  117.4 4.3 copy-start.9
  127.2 4.8 copy-start.4
  127.2 4.8 copy-start.22
  133.4 1.6 copy-start.15
  133.4 1.6 copy-start.23
  133.4 1.6 copy-start.30
  135.0 1.4 copy-start.17
  136.3 1.7 copy-start.35
  136.3 2.3 copy-start.12
  145.4 1.3 copy-start.5
  150.1 120.5 %reduce-scatter.3.cloned.1.call-start = ((), (), s32[]{:S(2)}) async-start(), calls=%async_computation.2 | async-start | bytes 7864320 | tf_op jit(solution)/shard_map/reduce_scatter | solution.py:106
  164.2 2.7 copy-start.33
  177.1 4.5 copy-start.11
  181.6 1.9 copy-start
  183.5 2.7 copy-start.6
  194.3 2.8 copy-start.8
  207.5 122.7 %all-gather.8.cloned.1.call-start = ((), (), s32[]{:S(2)}) async-start(), calls=%async_computation.5 | async-start | bytes 2162688 | tf_op jit(solution)/shard_map/all_gather | solution.py:125
  207.7 3.5 copy-start.3
  207.8 3.5 copy-start.7
  211.3 1.6 copy-start.14
  211.3 1.8 copy-start.34
  217.7 243.8 %all-reduce.3.cloned.1.call-start = ((), (), s32[]{:S(2)}) async-start(), calls=%async_computation.6 | async-start | bytes 6291456 | tf_op jit(solution)/shard_map/psum | solution.py:107
  270.6 4.4 copy-start.13
  270.7 4.4 copy-start.32
  270.7 4.4 copy-start.36
  463.2 2.4 copy-start.16
Sparse Core Ops, SparseCore 0:
  15.6 84.7 all-gather.5
  150.2 58.8 reduce-scatter.4
  211.7 58.8 reduce-scatter.2
  273.9 56.2 all-gather.7
  333.7 127.7 all-reduce.2
